TPU v7x, 128 devices: a whole 4x4x4 slice. The times are simulated.
128 devices in a mesh: pod: 1, data: 64 (over z, y, x), stage: 2 (over core).
Axes of the slice: x: 4, y: 4, z: 4, core: 2. Of those that a mesh axis runs over, the one named last changes fastest.
Arguments:
- token_ids: int32 [128, 256], P(('pod', 'data'))
- label_ids: int32 [128, 256], P(('pod', 'data'))
- embed_table: bfloat16 [32128, 768], replicated
- w_up: bfloat16 [2, 768, 3072], P('stage')
- w_down: bfloat16 [2, 3072, 768], P('stage')
Outputs:
- output 1: float32 [128], P(('pod', 'data'))
- output 2: float32 [32128, 768], P(('pod', 'data'))
- output 3: float32 [2, 768, 3072], P(('pod', 'stage'), 'data')
- output 4: float32 [2, 3072, 768], P(('pod', 'stage'), 'data')
All inputs are finite; a program needn't handle non-finite values.
Results may differ from a plain program's by a relative error of at most 0.00717123.
Values are sent between devices in bfloat16 or wider.
A program may use at most 1 GiB of HBM per device.

v0:
```python
import jax
import jax.numpy as jnp
from jax import lax
from jax.sharding import PartitionSpec as P

NORM_EPS = 1e-6


def layer_forward(state, w_one, w_two):
    hidden = jnp.dot(state, w_one, preferred_element_type=jnp.float32)
    gated = jax.nn.gelu(hidden).astype(jnp.bfloat16)
    mixed = jnp.dot(gated, w_two, preferred_element_type=jnp.float32)
    return (state.astype(jnp.float32) + mixed).astype(jnp.bfloat16)


def layer_backward(state, grad_out, w_one, w_two):
    hidden = jnp.dot(state, w_one, preferred_element_type=jnp.float32)
    gelu_out, gelu_pull = jax.vjp(jax.nn.gelu, hidden)
    gated = gelu_out.astype(jnp.bfloat16)
    grad_gated = jnp.einsum('td,fd->tf', grad_out, w_two, preferred_element_type=jnp.float32)
    grad_hidden = gelu_pull(grad_gated.astype(jnp.bfloat16).astype(jnp.float32))[0].astype(jnp.bfloat16)
    grad_two = jnp.einsum('tf,td->fd', gated, grad_out, preferred_element_type=jnp.float32)
    grad_one = jnp.einsum('td,tf->df', state, grad_hidden, preferred_element_type=jnp.float32)
    through_layer = jnp.einsum('tf,df->td', grad_hidden, w_one, preferred_element_type=jnp.float32)
    grad_in = (grad_out.astype(jnp.float32) + through_layer).astype(jnp.bfloat16)
    return grad_in, grad_one, grad_two


def head_backward(state, table, labels, scale):
    wide = state.astype(jnp.float32)
    inv_rms = lax.rsqrt(jnp.mean(wide * wide, axis=-1, keepdims=True) + NORM_EPS)
    normed_wide = wide * inv_rms
    normed = normed_wide.astype(jnp.bfloat16)
    logits = jnp.einsum('td,vd->tv', normed, table, preferred_element_type=jnp.float32) * scale
    log_norm = jax.nn.logsumexp(logits, axis=-1)
    hit = lax.broadcasted_iota(jnp.int32, logits.shape, 1) == labels[:, None]
    picked = jnp.sum(jnp.where(hit, logits, 0.0), axis=-1)
    probs = jnp.exp(logits - log_norm[:, None])
    grad_logits = (jnp.where(hit, probs - 1.0, probs) * scale).astype(jnp.bfloat16)
    head_grad = jnp.einsum('tv,td->vd', grad_logits, normed, preferred_element_type=jnp.float32)
    grad_normed = jnp.einsum('tv,vd->td', grad_logits, table, preferred_element_type=jnp.float32)
    grad_normed = grad_normed.astype(jnp.bfloat16).astype(jnp.float32)
    inner = jnp.mean(grad_normed * normed_wide, axis=-1, keepdims=True)
    grad_top = (inv_rms * (grad_normed - normed_wide * inner)).astype(jnp.bfloat16)
    return jnp.mean(log_norm - picked), head_grad, grad_top


def solution(mesh):
    stages = mesh.shape['stage']
    fwd_perm = [(sender, sender + 1) for sender in range(stages - 1)]
    bwd_perm = [(sender + 1, sender) for sender in range(stages - 1)]

    def stage_program(token_rows, label_rows, table, up_block, down_block):
        micro, seq_len = token_rows.shape
        vocab, width = table.shape
        w_one = up_block[0]
        w_two = down_block[0]
        scale = width ** -0.5
        stage_index = lax.axis_index('stage')
        is_first = stage_index == 0
        is_last = stage_index == stages - 1
        slots = min(micro, 2 * stages - 1)
        zero_rows = jnp.zeros((seq_len, width), jnp.bfloat16)

        def tick_body(tick_index, carry):
            from_prev, from_next, saved, sum_up, sum_down, sum_table, losses = carry
            fwd_index = tick_index - stage_index
            fwd_valid = (fwd_index >= 0) & (fwd_index < micro)
            fwd_index = jnp.clip(fwd_index, 0, micro - 1)
            tokens_now = lax.dynamic_index_in_dim(token_rows, fwd_index, 0, keepdims=False)
            labels_now = lax.dynamic_index_in_dim(label_rows, fwd_index, 0, keepdims=False)
            stage_input = jnp.where(is_first, table[tokens_now], from_prev)

            def run_fwd(store):
                return layer_forward(stage_input, w_one, w_two), lax.dynamic_update_index_in_dim(store, stage_input, fwd_index % slots, 0)

            def skip_fwd(store):
                return zero_rows, store

            stage_output, saved = lax.cond(fwd_valid, run_fwd, skip_fwd, saved)

            def run_head(state_pair):
                mean_ce, head_grad, grad_top = head_backward(stage_output, table, labels_now, scale)
                return state_pair[0] + head_grad, lax.dynamic_update_index_in_dim(state_pair[1], mean_ce, fwd_index, 0), grad_top

            def skip_head(state_pair):
                return state_pair[0], state_pair[1], zero_rows

            sum_table, losses, grad_top = lax.cond(is_last & fwd_valid, run_head, skip_head, (sum_table, losses))

            bwd_index = tick_index - (2 * stages - 2 - stage_index)
            bwd_valid = (bwd_index >= 0) & (bwd_index < micro)
            bwd_index = jnp.clip(bwd_index, 0, micro - 1)
            grad_out = jnp.where(is_last, grad_top, from_next)
            saved_input = lax.dynamic_index_in_dim(saved, bwd_index % slots, 0, keepdims=False)

            def run_bwd(grad_pair):
                grad_in, grad_one, grad_two = layer_backward(saved_input, grad_out, w_one, w_two)
                return grad_in, grad_pair[0] + grad_one, grad_pair[1] + grad_two

            def skip_bwd(grad_pair):
                return zero_rows, grad_pair[0], grad_pair[1]

            grad_in, sum_up, sum_down = lax.cond(bwd_valid, run_bwd, skip_bwd, (sum_up, sum_down))
            tokens_back = lax.dynamic_index_in_dim(token_rows, bwd_index, 0, keepdims=False)
            sum_table = lax.cond(is_first & bwd_valid,
                                 lambda table_sum: table_sum.at[tokens_back].add(grad_in.astype(jnp.float32)),
                                 lambda table_sum: table_sum, sum_table)
            from_prev = lax.ppermute(stage_output, 'stage', fwd_perm)
            from_next = lax.ppermute(grad_in, 'stage', bwd_perm)
            return from_prev, from_next, saved, sum_up, sum_down, sum_table, losses

        start = (zero_rows, zero_rows, jnp.zeros((slots, seq_len, width), jnp.bfloat16),
                 jnp.zeros(w_one.shape, jnp.float32), jnp.zeros(w_two.shape, jnp.float32),
                 jnp.zeros((vocab, width), jnp.float32), jnp.zeros((micro,), jnp.float32))
        final = lax.fori_loop(0, micro + 2 * stages - 2, tick_body, start)
        losses = lax.psum(jnp.where(is_last, final[6], 0.0), 'stage')
        grad_up = lax.psum_scatter(final[3], 'data', scatter_dimension=0, tiled=True)[None]
        grad_down = lax.psum_scatter(final[4], 'data', scatter_dimension=0, tiled=True)[None]
        grad_table = lax.psum(lax.psum_scatter(final[5], 'data', scatter_dimension=0, tiled=True), 'stage')
        return losses, grad_table, grad_up, grad_down

    rows_spec = P(('pod', 'data'), None)
    return jax.shard_map(stage_program, mesh=mesh,
                         in_specs=(rows_spec, rows_spec, P(None, None), P('stage', None, None), P('stage', None, None)),
                         out_specs=(P(('pod', 'data')), rows_spec, P(('pod', 'stage'), 'data', None), P(('pod', 'stage'), 'data', None)),
                         check_vma=False)
```

profile of v0, /device:TPU:7, one launch (start us, length us, event | category | flops | bytes accessed | tf_op | source)
XLA Modules:
  0.0 2004.6 jit_solution(13166014132108152740)
XLA Ops:
  8.0 31.0 %broadcast_in_dim.63 = f32[32128,768]{1,0:T(8,128)} broadcast(f32[]{:T(128)} %constant.226.clone.1), dimensions={} | broadcast | bytes 98697216 | tf_op jit(solution)/shard_map/broadcast_in_dim | solution.py:115
  49.6 467.3 %while.30 = (s32[]{:T(128)}, bf16[256,768]{1,0:T(8,128)(2,1)}, bf16[256,768]{1,0:T(8,128)(2,1)}, bf16[2,256,768]{2,1,0:T(8,128)(2,1)S(1)}, f32[768,3072]{1,0:T(8...) while((s32[]{:T(128)}, bf16[256,768]{1,0:T(8,128)(2,1)}, ...), condition=%wide.region_16.17_spmd, body=%wide.region_0.16_spmd.sunk | while | flops 46578663424 | bytes 655794304 | solution.py:116
  51.4 13.1 collective-permute-start.1
  68.1 11.5 conditional.8
  72.9 6.7 fusion.60
  79.7 153.0 %conditional.9 = (f32[32128,768]{1,0:T(8,128)}, f32[2]{0:T(128)S(1)}, bf16[256,768]{1,0:T(8,128)(2,1)S(1)}) conditional(s32[]{:T(128)} %convert_element_type.207, (f32[32128,768]{1,0:T(8,128)}, f32[2]{0:T(128)S(1)}) %tuple.125, (s32[2,256]{1,0:T(2,128)S(1)}, s32[]{:T(128)}, bf16[256,768]{1,0:T(8,128)(2,1)S(1)}, bf16[32128,768]{1,0:T(8,128)(2,1)}, ...), branch_computations={%region_3.3_spmd, %region_4.10_spmd} | conditional | flops 38084804608 | bytes 431648800 | solution.py:89
  79.9 32.5 %fusion.67 = (f32[256]{0:T(256)S(1)}, f32[256,32128]{1,0:T(8,128)}) fusion(bf16[32128,768]{1,0:T(8,128)(2,1)} %get-tuple-element.681, bf16[256,768]{1,0:T(8,128)(2,1)S(1)} %get-tuple-element.680, f32[256]{0:T(256)S(1)} %add_rsqrt_fusion), kind=kOutput, calls=%fused_computation.92 | convolution fusion | flops 12650283008 | bytes 82642944 | tf_op jit(solution)/shard_map/while/body/eval_jaxpr/cond/branch_1_fun/td,vd->tv/dot_general | solution.py:34
  112.3 16.2 select_reduce_fusion
  129.1 29.5 %fusion.8 = (f32[256]{0:T(256)S(1)}, f32[256,768]{1,0:T(8,128)S(1)}) fusion(bf16[256,768]{1,0:T(8,128)(2,1)S(1)} %get-tuple-element.680, f32[256]{0:T(256)S(1)} %add_rsqrt_fusion, bf16[32128,768]{1,0:T(8,128)(2,1)} %get-tuple-element.681, f32[256,32128]{1,0:T(8,128)} %get-tuple-element.781, f32[256]{0:T(256)S(1)} %get-tuple-element.777, s32[256]{0:T(256)S(1)} %bitcast.42), kind=kOutput, calls=%fused_computation.17 | convolution fusion | flops 12683771904 | bytes 83431424 | tf_op jit(solution)/shard_map/while/body/eval_jaxpr/cond/branch_1_fun/tv,vd->td/dot_general | solution.py:41
  158.9 73.0 %convolution_add_fusion = f32[32128,768]{1,0:T(8,128)} fusion(f32[32128,768]{1,0:T(8,128)} %get-tuple-element.677, bf16[256,768]{1,0:T(8,128)(2,1)S(1)} %get-tuple-element.680, f32[256]{0:T(256)S(1)} %add_rsqrt_fusion, f32[256,32128]{1,0:T(8,128)} %get-tuple-element.781, f32[256]{0:T(256)S(1)} %get-tuple-element.777, s32[256]{0:T(256)S(1)} %bitcast.43), kind=kOutput, calls=%fused_computation.2 | convolution fusion | flops 12707856384 | bytes 230689792 | tf_op jit(solution)/shard_map/while/body/eval_jaxpr/cond/branch_1_fun/tv,td->vd/dot_general | solution.py:40
  232.7 22.8 %conditional.10 = (bf16[256,768]{1,0:T(8,128)(2,1)}, f32[768,3072]{1,0:T(8,128)}, f32[3072,768]{1,0:T(8,128)}) conditional(s32[]{:T(128)} %convert_element_type.206, (f32[768,3072]{1,0:T(8,128)}, f32[3072,768]{1,0:T(8,128)}) %tuple.124, (pred[]{:T(512)}, bf16[256,768]{1,0:T(8,128)(2,1)S(1)}, bf16[256,768]{1,0:T(8,128)(2,1)S(1)}, ...), branch_computations={%region_11.11_spmd, %region_12.12_spmd} | conditional | flops 6069682176 | bytes 201720160 | solution.py:104
  247.5 7.9 fusion.31
  260.3 11.5 conditional.8
  265.1 6.7 fusion.60
  271.9 153.0 %conditional.9 = (f32[32128,768]{1,0:T(8,128)}, f32[2]{0:T(128)S(1)}, bf16[256,768]{1,0:T(8,128)(2,1)S(1)}) conditional(s32[]{:T(128)} %convert_element_type.207, (f32[32128,768]{1,0:T(8,128)}, f32[2]{0:T(128)S(1)}) %tuple.125, (s32[2,256]{1,0:T(2,128)S(1)}, s32[]{:T(128)}, bf16[256,768]{1,0:T(8,128)(2,1)S(1)}, bf16[32128,768]{1,0:T(8,128)(2,1)}, ...), branch_computations={%region_3.3_spmd, %region_4.10_spmd} | conditional | flops 38084804608 | bytes 431648800 | solution.py:89
  272.1 32.4 %fusion.67 = (f32[256]{0:T(256)S(1)}, f32[256,32128]{1,0:T(8,128)}) fusion(bf16[32128,768]{1,0:T(8,128)(2,1)} %get-tuple-element.681, bf16[256,768]{1,0:T(8,128)(2,1)S(1)} %get-tuple-element.680, f32[256]{0:T(256)S(1)} %add_rsqrt_fusion), kind=kOutput, calls=%fused_computation.92 | convolution fusion | flops 12650283008 | bytes 82642944 | tf_op jit(solution)/shard_map/while/body/eval_jaxpr/cond/branch_1_fun/td,vd->tv/dot_general | solution.py:34
  304.5 16.2 select_reduce_fusion
  321.3 29.5 %fusion.8 = (f32[256]{0:T(256)S(1)}, f32[256,768]{1,0:T(8,128)S(1)}) fusion(bf16[256,768]{1,0:T(8,128)(2,1)S(1)} %get-tuple-element.680, f32[256]{0:T(256)S(1)} %add_rsqrt_fusion, bf16[32128,768]{1,0:T(8,128)(2,1)} %get-tuple-element.681, f32[256,32128]{1,0:T(8,128)} %get-tuple-element.781, f32[256]{0:T(256)S(1)} %get-tuple-element.777, s32[256]{0:T(256)S(1)} %bitcast.42), kind=kOutput, calls=%fused_computation.17 | convolution fusion | flops 12683771904 | bytes 83431424 | tf_op jit(solution)/shard_map/while/body/eval_jaxpr/cond/branch_1_fun/tv,vd->td/dot_general | solution.py:41
  351.1 73.0 %convolution_add_fusion = f32[32128,768]{1,0:T(8,128)} fusion(f32[32128,768]{1,0:T(8,128)} %get-tuple-element.677, bf16[256,768]{1,0:T(8,128)(2,1)S(1)} %get-tuple-element.680, f32[256]{0:T(256)S(1)} %add_rsqrt_fusion, f32[256,32128]{1,0:T(8,128)} %get-tuple-element.781, f32[256]{0:T(256)S(1)} %get-tuple-element.777, s32[256]{0:T(256)S(1)} %bitcast.43), kind=kOutput, calls=%fused_computation.2 | convolution fusion | flops 12707856384 | bytes 230689792 | tf_op jit(solution)/shard_map/while/body/eval_jaxpr/cond/branch_1_fun/tv,td->vd/dot_general | solution.py:40
  424.8 22.8 %conditional.10 = (bf16[256,768]{1,0:T(8,128)(2,1)}, f32[768,3072]{1,0:T(8,128)}, f32[3072,768]{1,0:T(8,128)}) conditional(s32[]{:T(128)} %convert_element_type.206, (f32[768,3072]{1,0:T(8,128)}, f32[3072,768]{1,0:T(8,128)}) %tuple.124, (pred[]{:T(512)}, bf16[256,768]{1,0:T(8,128)(2,1)S(1)}, bf16[256,768]{1,0:T(8,128)(2,1)S(1)}, ...), branch_computations={%region_11.11_spmd, %region_12.12_spmd} | conditional | flops 6069682176 | bytes 201720160 | solution.py:104
  439.7 7.9 fusion.31
  454.3 59.0 %collective-permute-start.1 = (bf16[256,768]{1,0:T(8,128)(2,1)}, bf16[256,768]{1,0:T(8,128)(2,1)S(1)}, u32[]{:S(2)}, u32[]{:S(2)}) collective-permute-start(bf16[256,768]{1,0:T(8,128)(2,1)} %get-tuple-element.898), channel_id=1, source_target_pairs={{1,0},{3,2},{5,4},{7,6},{9,8},{11,10},{13,12},{15,14},{17,16},{19,... | collective-permute-start | bytes 1179656 | tf_op jit(solution)/shard_map/while/body/eval_jaxpr/ppermute | solution.py:110
  516.9 1049.1 %fusion = f32[512,768]{1,0:T(8,128)S(1)} fusion(f32[32128,768]{1,0:T(8,128)} %get-tuple-element.733), kind=kCustom, calls=%all-reduce-scatter | all-reduce-scatter fusion | flops 25165824 | bytes 100270592
  1575.4 10.8 collective-permute-done.3
  1586.3 23.3 %collective-permute-done.2 = f32[512,768]{1,0:T(8,128)S(1)} collective-permute-done((f32[512,768]{1,0:T(8,128)S(1)}, f32[512,768]{1,0:T(8,128)S(1)}, u32[]{:S(2)}, u32[]{:S(2)}) %collective-permute-start.2) | collective-permute-done | bytes 1572896
  1609.5 10.7 concatenate
  1623.5 190.2 %fusion.1 = f32[16,3072]{1,0:T(8,128)S(1)} fusion(f32[768,3072]{1,0:T(8,128)} %get-tuple-element.734), kind=kCustom, calls=%all-reduce-scatter.1 | all-reduce-scatter fusion | flops 3145729 | bytes 9634304
  1828.5 9.7 collective-permute-start.14
  1839.5 12.9 collective-permute-start.16
  1863.7 9.6 collective-permute-start.8
  1879.1 82.5 %psum.14 = f32[2]{0:T(128)} all-reduce(f32[2]{0:T(128)S(1)} %broadcast_select_fusion.2), channel_id=1, replica_groups=mesh['pod'=1,'data'=64,'stage'=2] {'stage'}, use_global_device_ids=true, to_apply=%region_17.18 | all-reduce | flops 2 | bytes 16 | tf_op jit(solution)/shard_map/psum | solution.py:117
  1963.7 30.0 %concatenate.1 = f32[268,3072]{1,0:T(8,128)S(1)} concatenate(f32[12,3072]{1,0:T(8,128)} %copy-done.4, f32[16,3072]{1,0:T(8,128)} %copy-done.13, f32[16,3072]{1,0:T(8,128)} %copy-done.12, f32[16,3072]{1,0:T(8,128)} %copy-done.11, f32[16,3072]{1,0:T(8,128)} %copy-done.10, f32[16,3072]{1,0:T(8,128)} %copy-done.9, f32[16,3072]{1,0:T(8,128)} %copy-done.8, f32[16,3072]{1,0:T(8,128)} %copy-done.7, ...), dimensions={0} | concatenate | bytes 6586368
  (201 shorter events, 123.6 us)
Async XLA Ops:
  8.0 1986.5 %all-reduce.6.cloned.1.call-start = ((), (), s32[]{:S(2)}) async-start(), calls=%async_computation.1 | async-start | bytes 3096576 | tf_op jit(solution)/shard_map/psum | solution.py:120
  51.4 14.4 collective-permute-start.1
  64.5 3.6 collective-permute-start
  79.7 153.0 %copy-start.2 = (bf16[256,768]{1,0:T(8,128)(2,1)S(1)}, bf16[256,768]{1,0:T(8,128)(2,1)}, u32[]{:S(2)}) copy-start(bf16[256,768]{1,0:T(8,128)(2,1)} %get-tuple-element.941) | copy-start | bytes 1179652 | tf_op jit(solution)/shard_map/while
  255.4 2.6 collective-permute-start.1
  256.7 3.6 collective-permute-start
  271.9 153.0 %copy-start.2 = (bf16[256,768]{1,0:T(8,128)(2,1)S(1)}, bf16[256,768]{1,0:T(8,128)(2,1)}, u32[]{:S(2)}) copy-start(bf16[256,768]{1,0:T(8,128)(2,1)} %get-tuple-element.941) | copy-start | bytes 1179652 | tf_op jit(solution)/shard_map/while
  447.6 2.6 collective-permute-start.1
  448.9 3.6 collective-permute-start
  454.3 60.4 %collective-permute-start.1 = (bf16[256,768]{1,0:T(8,128)(2,1)}, bf16[256,768]{1,0:T(8,128)(2,1)S(1)}, u32[]{:S(2)}, u32[]{:S(2)}) collective-permute-start(bf16[256,768]{1,0:T(8,128)(2,1)} %get-tuple-element.898), channel_id=1, source_target_pairs={{1,0},{3,2},{5,4},{7,6},{9,8},{11,10},{13,12},{15,14},{17,16},{19,... | collective-permute-start | bytes 1179656 | tf_op jit(solution)/shard_map/while/body/eval_jaxpr/ppermute | solution.py:110
  513.3 3.6 collective-permute-start
  516.9 1057.3 %copy-start.20 = (u32[128]{0:T(128)S(1)}, u32[128]{0:T(128)}, u32[]{:S(2)}) copy-start(u32[128]{0:T(128)} %constant.234) | copy-start | bytes 1540
  1566.0 43.6 %collective-permute-start.2 = (f32[512,768]{1,0:T(8,128)S(1)}, f32[512,768]{1,0:T(8,128)S(1)}, u32[]{:S(2)}, u32[]{:S(2)}) collective-permute-start(f32[512,768]{1,0:T(8,128)S(1)} %fusion), channel_id=1, source_target_pairs={{0,2},{2,4},{4,6},{6,8},{8,10},{10,12},{12,14},{14,16},{16,18},{18... | collective-permute-start | bytes 4718600
  1572.3 14.0 collective-permute-start.3
  1622.9 371.6 %reduce-scatter.6.cloned.1.call-start = ((), (), s32[]{:S(2)}) async-start(), calls=%async_computation.2 | async-start | bytes 9584640 | tf_op jit(solution)/shard_map/reduce_scatter | solution.py:119
  1813.8 14.7 collective-permute-start.19
  1815.1 23.1 %collective-permute-start.10 = (f32[16,3072]{1,0:T(8,128)S(1)}, f32[16,3072]{1,0:T(8,128)S(1)}, u32[]{:S(2)}, u32[]{:S(2)}) collective-permute-start(f32[16,3072]{1,0:T(8,128)S(1)} %fusion.1), channel_id=1, source_target_pairs={{0,14},{2,16},{4,18},{6,20},{8,22},{10,24},{12,26},{14,28},{16,30}... | collective-permute-start | bytes 589832
  1816.4 23.1 %collective-permute-start.11 = (f32[16,3072]{1,0:T(8,128)S(1)}, f32[16,3072]{1,0:T(8,128)S(1)}, u32[]{:S(2)}, u32[]{:S(2)}) collective-permute-start(f32[16,3072]{1,0:T(8,128)S(1)} %fusion.1), channel_id=1, source_target_pairs={{0,16},{2,18},{4,20},{6,22},{8,24},{10,26},{12,28},{14,30},{16,32}... | collective-permute-start | bytes 589832
  1821.6 30.9 %collective-permute-start.12 = (f32[16,3072]{1,0:T(8,128)S(1)}, f32[16,3072]{1,0:T(8,128)S(1)}, u32[]{:S(2)}, u32[]{:S(2)}) collective-permute-start(f32[16,3072]{1,0:T(8,128)S(1)} %fusion.1), channel_id=1, source_target_pairs={{0,18},{2,20},{4,22},{6,24},{8,26},{10,28},{12,30},{14,32},{16,34}... | collective-permute-start | bytes 589832
  1823.7 30.1 %collective-permute-start.13 = (f32[16,3072]{1,0:T(8,128)S(1)}, f32[16,3072]{1,0:T(8,128)S(1)}, u32[]{:S(2)}, u32[]{:S(2)}) collective-permute-start(f32[16,3072]{1,0:T(8,128)S(1)} %fusion.1), channel_id=1, source_target_pairs={{0,20},{2,22},{4,24},{6,26},{8,28},{10,30},{12,32},{14,34},{16,36}... | collective-permute-start | bytes 589832
  1828.5 44.9 %copy-start.4 = (f32[12,3072]{1,0:T(8,128)}, f32[12,3072]{1,0:T(8,128)S(1)}, u32[]{:S(2)}) copy-start(f32[12,3072]{1,0:T(8,128)S(1)} %collective-permute-done.19) | copy-start | bytes 442372
  1828.5 26.7 %collective-permute-start.14 = (f32[16,3072]{1,0:T(8,128)S(1)}, f32[16,3072]{1,0:T(8,128)S(1)}, u32[]{:S(2)}, u32[]{:S(2)}) collective-permute-start(f32[16,3072]{1,0:T(8,128)S(1)} %fusion.1), channel_id=1, source_target_pairs={{0,22},{2,24},{4,26},{6,28},{8,30},{10,32},{12,34},{14,36},{16,38}... | collective-permute-start | bytes 589832
  1838.2 19.4 collective-permute-start.15
  1839.5 20.9 %collective-permute-start.16 = (f32[16,3072]{1,0:T(8,128)S(1)}, f32[16,3072]{1,0:T(8,128)S(1)}, u32[]{:S(2)}, u32[]{:S(2)}) collective-permute-start(f32[16,3072]{1,0:T(8,128)S(1)} %fusion.1), channel_id=1, source_target_pairs={{0,26},{2,28},{4,30},{6,32},{8,34},{10,36},{12,38},{14,40},{16,42}... | collective-permute-start | bytes 589832
  1852.5 9.9 collective-permute-start.17
  1853.8 9.9 collective-permute-start.18
  1855.1 18.2 collective-permute-start.4
  1857.6 104.6 %collective-permute-start.5 = (f32[16,3072]{1,0:T(8,128)S(1)}, f32[16,3072]{1,0:T(8,128)S(1)}, u32[]{:S(2)}, u32[]{:S(2)}) collective-permute-start(f32[16,3072]{1,0:T(8,128)S(1)} %fusion.1), channel_id=1, source_target_pairs={{0,4},{2,6},{4,8},{6,10},{8,12},{10,14},{12,16},{14,18},{16,20},{1... | collective-permute-start | bytes 589832
  1860.5 101.8 %collective-permute-start.6 = (f32[16,3072]{1,0:T(8,128)S(1)}, f32[16,3072]{1,0:T(8,128)S(1)}, u32[]{:S(2)}, u32[]{:S(2)}) collective-permute-start(f32[16,3072]{1,0:T(8,128)S(1)} %fusion.1), channel_id=1, source_target_pairs={{0,6},{2,8},{4,10},{6,12},{8,14},{10,16},{12,18},{14,20},{16,22},{... | collective-permute-start | bytes 589832
  1862.4 99.8 %collective-permute-start.7 = (f32[16,3072]{1,0:T(8,128)S(1)}, f32[16,3072]{1,0:T(8,128)S(1)}, u32[]{:S(2)}, u32[]{:S(2)}) collective-permute-start(f32[16,3072]{1,0:T(8,128)S(1)} %fusion.1), channel_id=1, source_target_pairs={{0,8},{2,10},{4,12},{6,14},{8,16},{10,18},{12,20},{14,22},{16,24},... | collective-permute-start | bytes 589832
  1863.7 98.5 %collective-permute-start.8 = (f32[16,3072]{1,0:T(8,128)S(1)}, f32[16,3072]{1,0:T(8,128)S(1)}, u32[]{:S(2)}, u32[]{:S(2)}) collective-permute-start(f32[16,3072]{1,0:T(8,128)S(1)} %fusion.1), channel_id=1, source_target_pairs={{0,10},{2,12},{4,14},{6,16},{8,18},{10,20},{12,22},{14,24},{16,26}... | collective-permute-start | bytes 589832
  1873.3 90.4 %collective-permute-start.9 = (f32[16,3072]{1,0:T(8,128)S(1)}, f32[16,3072]{1,0:T(8,128)}, u32[]{:S(2)}, u32[]{:S(2)}) collective-permute-start(f32[16,3072]{1,0:T(8,128)S(1)} %fusion.1), channel_id=1, source_target_pairs={{0,12},{2,14},{4,16},{6,18},{8,20},{10,22},{12,24},{14,26},{16,28}... | collective-permute-start | bytes 589832
  (37 other events, 356.9 us)
Sparse Core Ops, SparseCore 0:
  1623.0 89.1 all-reduce.5
Sparse Core Ops, SparseCore 1:
  1628.5 350.2 reduce-scatter.5
where the time goes:
time: 2010 us; the launch traced here: 2000 us
  blocking collectives  1320 us (66%)
  matrix products  328 us (16%)
  starting transfers between devices  152 us (8%)
  local copies, waits for them, and re-layouts  101 us (5%)
  waiting for transfers between devices  44.2 us (2%)
  other arithmetic  38.1 us (2%)
    unnamed x2, blocking collectives  1240 us
    dot_general x2, matrix products, head_backward(): jnp.einsum('tv,td->vd', grad_logits, normed, preferred_element_type=jnp.f...  146 us
    psum x1, blocking collectives, stage_program(): losses = lax.psum(jnp.where(is_last, final[6], 0.0), 'stage')  82.5 us
    ppermute x4, starting transfers between devices, tick_body(): from_next = lax.ppermute(grad_in, 'stage', bwd_perm)  74.7 us
    unnamed x18, starting transfers between devices  72.4 us
    dot_general x2, matrix products, head_backward(): jnp.einsum('td,vd->tv', normed, table, preferred_element_type=jnp.float32)  64.9 us
    dot_general x2, matrix products, head_backward(): jnp.einsum('tv,vd->td', grad_logits, table, preferred_element_type=jnp.fl...  59 us
    unnamed x42, local copies, waits for them, and re-layouts  48.9 us
  transfers between devices with their start and end apart: 28, of which 7 were waited for; matrix products, arithmetic and copies ran while one was open for 11% of the time, Pallas kernels for 0%

commit v1 on v0

v1 whole, which is shorter than its diff:
```python
import functools
import math

import jax
import jax.numpy as jnp
from jax import lax
from jax.experimental import pallas as pl
from jax.experimental.pallas import tpu as pltpu
from jax.sharding import PartitionSpec as P

NORM_EPS = 1e-6
BF = jnp.bfloat16
F32 = jnp.float32
VOCAB = 32128
DIM = 768
FFN = 3072
SEQ = 256
CHUNK = 768
NCH = FFN // CHUNK
ROWS = 502
WIN = 528
HALF = WIN // 2
SCALE = DIM ** -0.5
LOG2E = math.log2(math.e)
C2 = SCALE * LOG2E
GC = math.sqrt(2.0 / math.pi)
GA = 0.044715
VBLK = 2048
VSUB = 512
TBLK = 1024

NT = (((1,), (1,)), ((), ()))
NN = (((1,), (0,)), ((), ()))


def dot(a, b, dims):
    return lax.dot_general(a, b, dims, preferred_element_type=F32)


def gelu(h):
    return 0.5 * h * (1.0 + jnp.tanh(GC * (h + GA * h * h * h)))


def gelu_grad(h):
    t = jnp.tanh(GC * (h + GA * h * h * h))
    return 0.5 * (1.0 + t) + 0.5 * h * (1.0 - t * t) * (GC * (1.0 + 3.0 * GA * h * h))


def any_spec():
    return pl.BlockSpec(memory_space=pl.ANY)


def weight_copies(me, own_up, own_dn, oth_up, oth_dn, up_buf, dn_buf, sems):
    def up(ref, s, j):
        return pltpu.make_async_copy(ref.at[:, pl.ds(j * CHUNK, CHUNK)], up_buf.at[s, j], sems.at[s, j, 0])

    def dn(ref, s, j):
        return pltpu.make_async_copy(ref.at[pl.ds(j * CHUNK, CHUNK), :], dn_buf.at[s, j], sems.at[s, j, 1])

    def start(s, j):
        @pl.when(me == s)
        def _():
            up(own_up, s, j).start()
            dn(own_dn, s, j).start()

        @pl.when(me != s)
        def _():
            up(oth_up, s, j).start()
            dn(oth_dn, s, j).start()

    def wait(s, j):
        up(own_up, s, j).wait()
        dn(own_dn, s, j).wait()

    return start, wait


def fwd_kernel(me_ref, x_ref, own_up, own_dn, oth_up, oth_dn, x1_ref, x2_ref, n_ref, h_ref, up_buf, dn_buf, sems):
    start, wait = weight_copies(me_ref[0], own_up, own_dn, oth_up, oth_dn, up_buf, dn_buf, sems)
    for s in range(2):
        for j in range(NCH):
            start(s, j)
    x = x_ref[...]
    for s in range(2):
        acc = x.astype(F32)
        for j in range(NCH):
            wait(s, j)
            h = dot(x, up_buf[s, j], NN)
            h_ref[s, :, j * CHUNK:(j + 1) * CHUNK] = h
            acc = acc + dot(gelu(h).astype(BF), dn_buf[s, j], NN)
        x = acc.astype(BF)
        (x1_ref, x2_ref)[s][...] = x
    wide = x.astype(F32)
    inv = lax.rsqrt(jnp.mean(wide * wide, axis=-1, keepdims=True) + NORM_EPS)
    n_ref[...] = (wide * inv).astype(BF)


def bwd_kernel(me_ref, g_ref, h_ref, own_up, own_dn, oth_up, oth_dn, g1_ref, g0_ref, up_buf, dn_buf, sems):
    start, wait = weight_copies(me_ref[0], own_up, own_dn, oth_up, oth_dn, up_buf, dn_buf, sems)
    for s in (1, 0):
        for j in range(NCH):
            start(s, j)
    g = g_ref[...]
    for s in (1, 0):
        acc = g.astype(F32)
        for j in range(NCH):
            wait(s, j)
            gg = dot(g, dn_buf[s, j], NT).astype(BF).astype(F32)
            gh = (gg * gelu_grad(h_ref[s, :, j * CHUNK:(j + 1) * CHUNK])).astype(BF)
            acc = acc + dot(gh, up_buf[s, j], NT)
        g = acc.astype(BF)
        (g0_ref, g1_ref)[s][...] = g


def head_kernel(n_ref, lab_ref, el_ref, x2_ref, e_ref, gtop_ref, lse_ref, ce_ref, acc_ref, m_ref, s_ref, pk_ref):
    step = pl.program_id(0)
    last = pl.num_programs(0) - 1

    @pl.when(step == 0)
    def _():
        pk = jnp.sum(n_ref[...].astype(F32) * el_ref[...].astype(F32), axis=-1, keepdims=True) * C2
        pk_ref[...] = jnp.broadcast_to(pk, pk_ref.shape)
        m_ref[...] = jnp.broadcast_to(pk, m_ref.shape)
        s_ref[...] = jnp.zeros_like(s_ref)
        acc_ref[...] = jnp.zeros_like(acc_ref)

    def run(rows):
        n = n_ref[...]
        rel = lab_ref[...] - step * VBLK
        m = m_ref[:, :1]
        s = s_ref[:, :1]
        for lo in range(0, rows, VSUB):
            width = min(VSUB, rows - lo)
            e = e_ref[lo:lo + width, :]
            l = dot(n, e, NT)
            new = jnp.maximum(m, jnp.max(l, axis=-1, keepdims=True) * C2)
            p = jnp.exp2(l * C2 - new)
            hit = lax.broadcasted_iota(jnp.int32, (SEQ, width), 1) + lo == rel
            p = jnp.where(hit, 0.0, p)
            alpha = jnp.exp2(m - new)
            s = s * alpha + jnp.sum(p, axis=-1, keepdims=True)
            acc_ref[...] = acc_ref[...] * alpha + dot(p.astype(BF), e, NN)
            m = new
        m_ref[...] = jnp.broadcast_to(m, m_ref.shape)
        s_ref[...] = jnp.broadcast_to(s, s_ref.shape)

    @pl.when(step != last)
    def _():
        run(VBLK)

    @pl.when(step == last)
    def _():
        run(VOCAB % VBLK)
        m = m_ref[:, :1]
        s = s_ref[:, :1]
        pk = pk_ref[:, :1]
        total = s + jnp.exp2(pk - m)
        lse2 = m + jnp.log2(total)
        lse_ref[...] = lse2
        ce_ref[...] = (lse2 - pk) * (1.0 / LOG2E)
        inv_total = 1.0 / total
        gn = (acc_ref[...] * inv_total - (s * inv_total) * el_ref[...].astype(F32)) * SCALE
        gn = gn.astype(BF).astype(F32)
        wide = x2_ref[...].astype(F32)
        inv = lax.rsqrt(jnp.mean(wide * wide, axis=-1, keepdims=True) + NORM_EPS)
        nw = wide * inv
        inner = jnp.mean(gn * nw, axis=-1, keepdims=True)
        gtop_ref[...] = (inv * (gn - nw * inner)).astype(BF)


def headgrad_kernel(a_ref, table_ref, n_ref, lse_ref, lab_ref, out_ref, e_buf, sems):
    step = pl.program_id(0)

    def copy(seg):
        src = table_ref.at[pl.ds(pl.multiple_of(a_ref[seg], 16), WIN), :]
        return pltpu.make_async_copy(src, e_buf.at[seg], sems.at[seg])

    @pl.when(step == 0)
    def _():
        for seg in range(4):
            copy(seg).start()
        out_ref[...] = jnp.zeros_like(out_ref)
        for seg in range(4):
            copy(seg).wait()

    n = n_ref[...]
    lse = lse_ref[...] - math.log2(SCALE)
    lab = lab_ref[...]
    row = lax.broadcasted_iota(jnp.int32, (WIN, TBLK), 0)
    for seg in range(4):
        l = dot(e_buf[seg], n, NT)
        p = jnp.exp2(l * C2 - lse)
        g = (p - jnp.where(row == lab - a_ref[seg], SCALE, 0.0)).astype(BF)
        d = dot(g, n, NN)
        out_ref[0, seg] += d[:HALF]
        out_ref[1, seg] += d[HALF:]


def embgrad_kernel(a_ref, part_ref, g_ref, tok_ref, out_ref):
    step = pl.program_id(0)

    @pl.when(step == 0)
    def _():
        out_ref[...] = part_ref[...]

    g = g_ref[...]
    tok = tok_ref[...]
    row = lax.broadcasted_iota(jnp.int32, (WIN, TBLK), 0)
    for seg in range(4):
        hot = jnp.where(row == tok - a_ref[seg], 1.0, 0.0).astype(BF)
        d = dot(hot, g, NN)
        out_ref[0, seg] += d[:HALF]
        out_ref[1, seg] += d[HALF:]


def cost(flops, nbytes, trans=0):
    return pl.CostEstimate(flops=int(flops), bytes_accessed=int(nbytes), transcendentals=int(trans))


def call_fwd(me, x, own_up, own_dn, oth_up, oth_dn):
    tok = jax.ShapeDtypeStruct((SEQ, DIM), BF)
    return pl.pallas_call(
        fwd_kernel,
        out_shape=(tok, tok, tok, jax.ShapeDtypeStruct((2, SEQ, FFN), F32)),
        in_specs=[pl.BlockSpec(memory_space=pltpu.SMEM), pl.BlockSpec(memory_space=pltpu.VMEM)] + [any_spec()] * 4,
        out_specs=[pl.BlockSpec(memory_space=pltpu.VMEM)] * 4,
        scratch_shapes=[pltpu.VMEM((2, NCH, DIM, CHUNK), BF), pltpu.VMEM((2, NCH, CHUNK, DIM), BF), pltpu.SemaphoreType.DMA((2, NCH, 2))],
        cost_estimate=cost(8 * SEQ * DIM * FFN, 26e6),
        name='fwd')(me, x, own_up, own_dn, oth_up, oth_dn)


def call_bwd(me, g, h, own_up, own_dn, oth_up, oth_dn):
    tok = jax.ShapeDtypeStruct((SEQ, DIM), BF)
    return pl.pallas_call(
        bwd_kernel,
        out_shape=(tok, tok),
        in_specs=[pl.BlockSpec(memory_space=pltpu.SMEM)] + [pl.BlockSpec(memory_space=pltpu.VMEM)] * 2 + [any_spec()] * 4,
        out_specs=[pl.BlockSpec(memory_space=pltpu.VMEM)] * 2,
        scratch_shapes=[pltpu.VMEM((2, NCH, DIM, CHUNK), BF), pltpu.VMEM((2, NCH, CHUNK, DIM), BF), pltpu.SemaphoreType.DMA((2, NCH, 2))],
        cost_estimate=cost(8 * SEQ * DIM * FFN, 26e6),
        name='bwd')(me, g, h, own_up, own_dn, oth_up, oth_dn)


def call_head(n, lab, el, x2, table):
    full = lambda shape: pl.BlockSpec(shape, lambda i: (0, 0))
    return pl.pallas_call(
        head_kernel,
        grid=(pl.cdiv(VOCAB, VBLK),),
        out_shape=(jax.ShapeDtypeStruct((SEQ, DIM), BF), jax.ShapeDtypeStruct((SEQ, 1), F32), jax.ShapeDtypeStruct((SEQ, 1), F32)),
        in_specs=[full((SEQ, DIM)), full((SEQ, 1)), full((SEQ, DIM)), full((SEQ, DIM)), pl.BlockSpec((VBLK, DIM), lambda i: (i, 0))],
        out_specs=(full((SEQ, DIM)), full((SEQ, 1)), full((SEQ, 1))),
        scratch_shapes=[pltpu.VMEM((SEQ, DIM), F32)] + [pltpu.VMEM((SEQ, 128), F32)] * 3,
        cost_estimate=cost(4 * SEQ * DIM * VOCAB, VOCAB * DIM * 2, SEQ * VOCAB),
        name='head')(n, lab, el, x2, table)


def call_headgrad(starts, table, n_all, lse_all, lab_all):
    toks = n_all.shape[0]
    return pl.pallas_call(
        headgrad_kernel,
        grid=(toks // TBLK,),
        out_shape=jax.ShapeDtypeStruct((2, 4, HALF, DIM), F32),
        in_specs=[pl.BlockSpec(memory_space=pltpu.SMEM), any_spec(), pl.BlockSpec((TBLK, DIM), lambda i: (i, 0)),
                  pl.BlockSpec((1, TBLK), lambda i: (0, i)), pl.BlockSpec((1, TBLK), lambda i: (0, i))],
        out_specs=pl.BlockSpec((2, 4, HALF, DIM), lambda i: (0, 0, 0, 0)),
        scratch_shapes=[pltpu.VMEM((4, WIN, DIM), BF), pltpu.SemaphoreType.DMA((4,))],
        cost_estimate=cost(4 * 4 * WIN * DIM * toks, 16e6, 4 * WIN * toks),
        name='headgrad')(starts, table, n_all, lse_all, lab_all)


def call_embgrad(starts, part, g_all, tok_all):
    toks = g_all.shape[0]
    shape = (2, 4, HALF, DIM)
    return pl.pallas_call(
        embgrad_kernel,
        grid=(toks // TBLK,),
        out_shape=jax.ShapeDtypeStruct(shape, F32),
        in_specs=[pl.BlockSpec(memory_space=pltpu.SMEM), pl.BlockSpec(shape, lambda i: (0, 0, 0, 0)),
                  pl.BlockSpec((TBLK, DIM), lambda i: (i, 0)), pl.BlockSpec((1, TBLK), lambda i: (0, i))],
        out_specs=pl.BlockSpec(shape, lambda i: (0, 0, 0, 0)),
        cost_estimate=cost(2 * 4 * WIN * DIM * toks, 20e6),
        name='embgrad')(starts, part, g_all, tok_all)


SWAP = [(0, 1), (1, 0)]


def gather_z(v):
    parts = [v]
    for k in (1, 3, 2):
        parts.append(lax.ppermute(v, 'z', [(i, (i + k) % 4) for i in range(4)]))
    return jnp.concatenate(parts, axis=0)


def step_program(token_rows, label_rows, table, up_block, down_block):
    me = lax.axis_index('stage')
    iz, iy, ix = lax.axis_index('z'), lax.axis_index('y'), lax.axis_index('x')
    own_up, own_dn = up_block[0], down_block[0]
    oth_up = lax.ppermute(own_up, 'stage', SWAP)
    oth_dn = lax.ppermute(own_dn, 'stage', SWAP)
    me1 = me.reshape(1).astype(jnp.int32)
    tok = lax.dynamic_index_in_dim(token_rows, me, 0, keepdims=False)
    lab = lax.dynamic_index_in_dim(label_rows, me, 0, keepdims=False)
    rows = table[jnp.concatenate([tok, lab])]
    x0, el = rows[:SEQ], rows[SEQ:]
    x1, x2, n, h = call_fwd(me1, x0, own_up, own_dn, oth_up, oth_dn)
    n_all = lax.all_gather(n, ('y', 'x'), axis=0, tiled=True)
    x_own = jnp.where(me == 0, x0, x1)
    x_oth = lax.ppermute(jnp.where(me == 0, x1, x0), 'stage', SWAP)
    x_g = gather_z(jnp.concatenate([x_own, x_oth], axis=0))
    gtop, lse, ce = call_head(n, lab[:, None], el, x2, table)
    g1, g0 = call_bwd(me1, gtop, h, own_up, own_dn, oth_up, oth_dn)
    g_all = lax.all_gather(g0, ('y', 'x'), axis=0, tiled=True)
    small = jnp.stack([lse[:, 0], lab.astype(F32), tok.astype(F32)])
    small = lax.all_gather(small, ('y', 'x'), axis=1, tiled=True)
    lse_all = small[0:1]
    lab_all = small[1:2].astype(jnp.int32)
    tok_all = small[2:3].astype(jnp.int32)

    owner = (jnp.arange(4, dtype=jnp.int32) * 4 + iy) * 4 + ix
    starts = jnp.minimum(owner * ROWS // 16 * 16, VOCAB - WIN)
    part = call_headgrad(starts, table, n_all, lse_all, lab_all)

    go_own = jnp.where(me == 0, g1, gtop)
    go_oth = lax.ppermute(jnp.where(me == 0, gtop, g1), 'stage', SWAP)
    go_g = gather_z(jnp.concatenate([go_own, go_oth], axis=0))
    up_sl = lax.dynamic_slice_in_dim(own_up, iz * CHUNK, CHUNK, 1)
    dn_sl = lax.dynamic_slice_in_dim(own_dn, iz * CHUNK, CHUNK, 0)
    hid = dot(x_g, up_sl, NN)
    gg = dot(go_g, dn_sl, NT).astype(BF).astype(F32)
    gated = gelu(hid).astype(BF)
    gh = (gg * gelu_grad(hid)).astype(BF)
    d_dn = lax.dot_general(gated, go_g, (((0,), (0,)), ((), ())), preferred_element_type=F32)
    d_up = lax.dot_general(x_g, gh, (((0,), (0,)), ((), ())), preferred_element_type=F32)
    d_up = d_up.reshape(4, 16, 12, CHUNK).transpose(1, 0, 2, 3).reshape(16, 48, CHUNK)
    d_w = jnp.concatenate([d_up, d_dn.reshape(16, 48, DIM)], axis=1).reshape(16 * 96, DIM)
    d_w = lax.psum_scatter(d_w, ('y', 'x'), scatter_dimension=0, tiled=True)
    grad_down = d_w[48:][None]
    up_parts = lax.all_to_all(d_w[:48].reshape(4, 12, CHUNK), 'z', split_axis=0, concat_axis=0, tiled=True)
    grad_up = up_parts.transpose(1, 0, 2).reshape(1, 12, FFN)

    part = call_embgrad(starts, part, g_all, tok_all)
    part = lax.psum_scatter(part, 'stage', scatter_dimension=0, tiled=True)[0]
    mine = lax.psum_scatter(part, 'z', scatter_dimension=0, tiled=True)[0]
    both = lax.all_gather(mine, 'stage', axis=0, tiled=True)
    my_owner = (iz * 4 + iy) * 4 + ix
    my_start = jnp.minimum(my_owner * ROWS // 16 * 16, VOCAB - WIN)
    grad_table = lax.dynamic_slice_in_dim(both, my_owner * ROWS - my_start, ROWS, 0)

    loss = jnp.mean(ce).reshape(1)
    losses = lax.all_gather(loss, 'stage', axis=0, tiled=True)
    return losses, grad_table, grad_up, grad_down


def solution(mesh):
    fine = jax.sharding.Mesh(mesh.devices.reshape(1, 4, 4, 4, 2), ('pod', 'z', 'y', 'x', 'stage'))
    data = ('z', 'y', 'x')
    rows_spec = P(('pod',) + data, None)
    return jax.shard_map(step_program, mesh=fine,
                         in_specs=(rows_spec, rows_spec, P(None, None), P('stage', None, None), P('stage', None, None)),
                         out_specs=(P(('pod',) + data), rows_spec, P(('pod', 'stage'), data, None), P(('pod', 'stage'), data, None)),
                         check_vma=False)
```

time: 2010 us -> 465 us (0.23)
  blocking collectives: 1320 us -> 24.6 us
  matrix products: 328 us -> 27.8 us
  waiting for transfers between devices: 44.2 us -> 190 us
  Pallas kernels: 0 us -> 143 us
  starting transfers between devices: 152 us -> 16.5 us
  local copies, waits for them, and re-layouts: 101 us -> 34.9 us
  other arithmetic: 38.1 us -> 5.94 us
    unnamed x2 -> x1, blocking collectives: 1240 us -> 6.04 us
    dot_general x18 -> x3, matrix products: 328 us -> 27.8 us  [the longest x1 15.6 us: step_program(): lax.dot_general(x_g, gh, (((0,), (0,)), ((), ())), preferred_element_type...]
    pallas_call x0 -> x5, Pallas kernels: none -> 143 us  [the longest x1 60.7 us: call_head(): pl.pallas_call(head_kernel, grid=(pl.cdiv(VOCAB, VBLK),), out_shape=(jax....]
    reduce_scatter x1 -> x3, waiting for transfers between devices: 0.01 us -> 95.7 us  [the longest x1 79.3 us: step_program(): d_w = lax.psum_scatter(d_w, ('y', 'x'), scatter_dimension=0, tiled=True)]
    psum x1 -> x0, blocking collectives: 82.5 us -> none  [stage_program(): losses = lax.psum(jnp.where(is_last, final[6], 0.0), 'stage')]
    ppermute x8 -> x10, waiting for transfers between devices: 8.89 us -> 85.5 us  [the longest x6 75.4 us: gather_z(): parts.append(lax.ppermute(v, 'z', [(i, (i + k) % 4) for i in range(4)]))]
    unnamed x18 -> x0, starting transfers between devices: 72.4 us -> none
    ppermute x8 -> x10, starting transfers between devices: 79.9 us -> 11.8 us  [the longest x6 10.3 us: gather_z(): parts.append(lax.ppermute(v, 'z', [(i, (i + k) % 4) for i in range(4)]))]
  transfers between devices with their start and end apart: 28 -> 17, of which waited for: 7 -> 12; matrix products, arithmetic and copies ran while one was open for 11% -> 14% of each run, Pallas kernels for 0% -> 24%
where the time goes in v1:
time: 465 us; the launch traced here: 458 us
  waiting for transfers between devices  190 us (41%)
  Pallas kernels  143 us (31%)
  local copies, waits for them, and re-layouts  34.9 us (8%)
  matrix products  27.8 us (6%)
  blocking collectives  24.6 us (5%)
  starting transfers between devices  16.5 us (4%)
  between operations  15.4 us (3%)
  other arithmetic  5.94 us (1%)
    reduce_scatter x1, waiting for transfers between devices, step_program(): d_w = lax.psum_scatter(d_w, ('y', 'x'), scatter_dimension=0, tiled=True)  79.3 us
    ppermute x6, waiting for transfers between devices, gather_z(): parts.append(lax.ppermute(v, 'z', [(i, (i + k) % 4) for i in range(4)]))  75.4 us
    pallas_call x1, Pallas kernels, call_head(): pl.pallas_call(head_kernel, grid=(pl.cdiv(VOCAB, VBLK),), out_shape=(jax....  60.7 us
    pallas_call x1, Pallas kernels, call_headgrad(): pl.pallas_call(headgrad_kernel, grid=(toks // TBLK,), out_shape=jax.Shape...  35 us
    pallas_call x1, Pallas kernels, call_embgrad(): pl.pallas_call(embgrad_kernel, grid=(toks // TBLK,), out_shape=jax.ShapeD...  20.7 us
    all_gather x1, blocking collectives, step_program(): small = lax.all_gather(small, ('y', 'x'), axis=1, tiled=True)  18.6 us
    reduce_scatter x1, waiting for transfers between devices, step_program(): part = lax.psum_scatter(part, 'stage', scatter_dimension=0, tiled=True)[0]  16.5 us
    dot_general x1, matrix products, step_program(): lax.dot_general(x_g, gh, (((0,), (0,)), ((), ())), preferred_element_type...  15.6 us
  transfers between devices with their start and end apart: 17, of which 12 were waited for; matrix products, arithmetic and copies ran while one was open for 14% of the time, Pallas kernels for 24%

profile of v1, /device:TPU:7, one launch (start us, length us, event | category | flops | bytes accessed | tf_op | source)
XLA Modules:
  0.0 458.3 jit_solution(8662290760363851171)
XLA Ops:
  8.8 4.1 gather_fusion
  13.7 1.8 collective-permute-done.oth_up
  15.5 6.7 %collective-permute-done.1.oth_dn = bf16[3072,768]{1,0:T(8,128)(2,1)} collective-permute-done((bf16[3072,768]{1,0:T(8,128)(2,1)}, bf16[3072,768]{1,0:T(8,128)(2,1)}, u32[]{:S(2)}, u32[]{:S(2)}) %collective-permute-start.1) | collective-permute-done | bytes 4718624 | tf_op jit(solution)/shard_map/ppermute | solution.py:300
  22.3 12.5 %fwd.1 = (bf16[256,768]{1,0:T(8,128)(2,1)}, bf16[256,768]{1,0:T(8,128)(2,1)}, bf16[256,768]{1,0:T(8,128)(2,1)}, f32[2,256,3072]{2,1,0:T(8,128)}) custom-call(s32[1]{0:T(128)} %bitcast.me_ref, bf16[256,768]{1,0:T(8,128)(2,1)} %slice.30.x_ref, bf16[768,3072]{1,0:T(8,128)(2,1)} %bitcast.34, bf16[3072,768]{1,0:T(8,128)(2,1)} %bitcast.37, ...), custom_call_target="tpu_custom_call" | custom-call | flops 4831838208 | bytes 26000000 | tf_op jit(solution)/shard_map/fwd/pallas_call | solution.py:222
  35.9 2.0 constant_dynamic-update-slice_fusion.4
  37.9 60.7 %head.1 = (bf16[256,768]{1,0:T(8,128)(2,1)}, f32[256,1]{1,0:T(8,128)}, f32[256,1]{1,0:T(8,128)}) custom-call(bf16[256,768]{1,0:T(8,128)(2,1)} %get-tuple-element.13.n_ref, s32[256,1]{1,0:T(8,128)} %copy.13.lab_ref, bf16[256,768]{1,0:T(8,128)(2,1)} %get-tuple-element.31.el_ref, bf16[256,768]{1,0:T(8,128)(2,1)} %get-tuple-element.14.x2_ref, ...), custom_call_target="tpu_custom_call" | custom-call | flops 25266487296 | bytes 49348608 | tf_op jit(solution)/shard_map/head/pallas_call | solution.py:246
  98.6 13.9 %bwd.1 = (bf16[256,768]{1,0:T(8,128)(2,1)}, bf16[256,768]{1,0:T(8,128)(2,1)}) custom-call(s32[1]{0:T(128)} %bitcast.me_ref, bf16[256,768]{1,0:T(8,128)(2,1)} %get-tuple-element.17.g_ref, f32[2,256,3072]{2,1,0:T(8,128)} %get-tuple-element.18.h_ref, bf16[768,3072]{1,0:T(8,128)(2,1)} %bitcast.35, bf16[3072,768]{1,0:T(8,128)(2,1)} %bitcast.38, ...), custom_call_target="tpu_custom_call" | custom-call | flops 4831838208 | bytes 26000000 | tf_op jit(solution)/shard_map/bwd/pallas_call | solution.py:234
  113.3 18.6 %all_gather.17 = f32[3,4096]{1,0:T(4,128)S(1)} all-gather(f32[3,256]{1,0:T(4,128)S(1)} %pad_maximum_fusion.3), channel_id=1, replica_groups=mesh['pod'=1,'z'=4,'y'=4,'x'=4,'stage'=2] {'y','x'}, dimensions={1}, use_global_device_ids=true | all-gather | bytes 52224 | tf_op jit(solution)/shard_map/all_gather | solution.py:315
  132.5 35.0 %headgrad.1.part_ref = f32[2,4,264,768]{3,2,1,0:T(8,128)} custom-call(s32[4]{0:T(128)} %multiply_minimum_fusion.a_ref, bf16[32128,768]{1,0:T(8,128)(2,1)} %table_ref.1, bf16[4096,768]{1,0:T(8,128)(2,1)} %all-gather.5.cloned.1.call-done.n_ref, f32[1,4096]{1,0:T(1,128)} %get-tuple-element.37.lse_ref, s32[1,4096]{1,0:T(1,128)} %get-tuple-element.36.lab_ref), custom_call_target="tpu_custom_call" | custom-call | flops 26575110144 | bytes 16000000 | tf_op jit(solution)/shard_map/headgrad/pallas_call | solution.py:259
  167.5 7.9 %all-gather.7.cloned.1.call-done.g_ref = bf16[4096,768]{1,0:T(8,128)(2,1)} async-done(((bf16[256,768]{1,0:T(8,128)(2,1)}), bf16[4096,768]{1,0:T(8,128)(2,1)}) %all-gather.7.cloned.1.call-update) | async-done | bytes 6291472 | tf_op jit(solution)/shard_map/all_gather | solution.py:313
  175.4 20.7 %embgrad.1 = f32[2,4,264,768]{3,2,1,0:T(8,128)} custom-call(s32[4]{0:T(128)} %multiply_minimum_fusion.a_ref, f32[2,4,264,768]{3,2,1,0:T(8,128)} %headgrad.1.part_ref, bf16[4096,768]{1,0:T(8,128)(2,1)} %all-gather.7.cloned.1.call-done.g_ref, s32[1,4096]{1,0:T(1,128)} %get-tuple-element.35.tok_ref), custom_call_target="tpu_custom_call" | custom-call | flops 13287555072 | bytes 20000000 | tf_op jit(solution)/shard_map/embgrad/pallas_call | solution.py:274
  196.2 16.5 %reduce-scatter.4.cloned.1.call-done = f32[1,4,264,768]{3,2,1,0:T(8,128)} async-done(((f32[2,4,264,768]{3,2,1,0:T(8,128)}), f32[1,4,264,768]{3,2,1,0:T(8,128)}) %reduce-scatter.4.cloned.1.call-update) | async-done | bytes 3244048 | tf_op jit(solution)/shard_map/reduce_scatter | solution.py:343
  220.8 2.5 collective-permute-start.8
  223.3 18.3 %collective-permute-done.3 = bf16[512,768]{1,0:T(8,128)(2,1)S(1)} collective-permute-done((bf16[512,768]{1,0:T(8,128)(2,1)S(1)}, bf16[512,768]{1,0:T(8,128)(2,1)S(1)}, u32[]{:S(2)}, u32[]{:S(2)}) %collective-permute-start.3) | collective-permute-done | bytes 786464 | tf_op jit(solution)/shard_map/ppermute | solution.py:291
  241.6 3.0 collective-permute-start.9
  247.1 2.1 constant_dynamic-update-slice_fusion.1
  249.1 25.5 %collective-permute-done.5 = bf16[512,768]{1,0:T(8,128)(2,1)} collective-permute-done((bf16[512,768]{1,0:T(8,128)(2,1)S(1)}, bf16[512,768]{1,0:T(8,128)(2,1)}, u32[]{:S(2)}, u32[]{:S(2)}) %collective-permute-start.5) | collective-permute-done | bytes 786464 | tf_op jit(solution)/shard_map/ppermute | solution.py:291
  274.7 2.1 constant_dynamic-update-slice_fusion
  276.8 15.6 %collective-permute-done.7 = bf16[512,768]{1,0:T(8,128)(2,1)} collective-permute-done((bf16[512,768]{1,0:T(8,128)(2,1)S(1)}, bf16[512,768]{1,0:T(8,128)(2,1)}, u32[]{:S(2)}, u32[]{:S(2)}) %collective-permute-start.7) | collective-permute-done | bytes 786464 | tf_op jit(solution)/shard_map/ppermute | solution.py:291
  292.4 2.1 constant_dynamic-update-slice_fusion.7
  294.5 1.7 collective-permute-done.8
  296.2 2.1 constant_dynamic-update-slice_fusion.6
  298.3 14.3 %collective-permute-done.9 = bf16[512,768]{1,0:T(8,128)(2,1)S(1)} collective-permute-done((bf16[512,768]{1,0:T(8,128)(2,1)S(1)}, bf16[512,768]{1,0:T(8,128)(2,1)S(1)}, u32[]{:S(2)}, u32[]{:S(2)}) %collective-permute-start.9) | collective-permute-done | bytes 786464 | tf_op jit(solution)/shard_map/ppermute | solution.py:291
  313.5 5.9 %fusion.11 = f32[2048,768]{1,0:T(8,128)} fusion(bf16[2048,768]{1,0:T(8,128)(2,1)S(1)} %copy-done.4, bf16[1,768,3072]{2,1,0:T(8,128)(2,1)} %param.8, s32[]{:T(128)S(6)} %select_n.62), kind=kOutput, calls=%fused_computation.17 | convolution fusion | flops 2415919104 | bytes 10616836 | tf_op jit(solution)/shard_map/dot_general | solution.py:37
  319.5 15.6 %fusion.9 = f32[768,768]{1,0:T(8,128)} fusion(bf16[2048,768]{1,0:T(8,128)(2,1)S(1)} %copy-done.5, f32[2048,768]{1,0:T(8,128)} %fusion.11, bf16[2048,768]{1,0:T(8,128)(2,1)} %constant_dynamic-update-slice_fusion.5, bf16[1,3072,768]{2,1,0:T(8,128)(2,1)} %param.9, s32[]{:T(128)S(6)} %select_n.62), kind=kOutput, calls=%fused_computation.15 | convolution fusion | flops 4864868352 | bytes 16121860 | tf_op jit(solution)/shard_map/dot_general | solution.py:334
  335.1 2.4 reshape.122
  338.9 6.3 %fusion.8 = f32[768,768]{1,0:T(8,128)S(1)} fusion(bf16[2048,768]{1,0:T(8,128)(2,1)} %constant_dynamic-update-slice_fusion.5, f32[2048,768]{1,0:T(8,128)} %fusion.11), kind=kOutput, calls=%fused_computation.14 | convolution fusion | flops 2430074880 | bytes 11796480 | tf_op jit(solution)/shard_map/dot_general | solution.py:333
  346.9 4.9 %copy.16 = f32[16,96,768]{2,1,0:T(8,128)} copy(f32[16,96,768]{2,0,1:T(8,128)S(1)} %pad_maximum_fusion) | data formatting | bytes 9437184 | tf_op jit(solution)/shard_map/concatenate | solution.py:336
  352.4 79.3 %reduce-scatter.8.cloned.1.call-done = f32[96,768]{1,0:T(8,128)} async-done(((f32[1536,768]{1,0:T(8,128)}), f32[96,768]{1,0:T(8,128)}) %reduce-scatter.8.cloned.1.call-update) | async-done | bytes 294928 | tf_op jit(solution)/shard_map/reduce_scatter | solution.py:337
  434.0 4.1 all-to-all-start
  440.7 6.0 %all-reduce = f32[2]{0:T(128)} all-reduce(f32[2]{0:T(128)S(1)} %dynamic-update-slice), channel_id=1, replica_groups=mesh['pod'=1,'z'=4,'y'=4,'x'=4,'stage'=2] {'stage'}, use_global_device_ids=true, to_apply=%add | all-reduce | flops 2 | bytes 16
  448.4 2.7 dynamic-slice_bitcast_fusion
  (68 shorter events, 26.2 us)
Async XLA Ops:
  7.2 125.3 %all-gather.5.cloned.1.call-start = ((), (), s32[]{:S(2)}) async-start(), calls=%async_computation.4 | async-start | bytes 6684672 | tf_op jit(solution)/shard_map/all_gather | solution.py:307
  7.2 8.3 %collective-permute-start = (bf16[768,3072]{1,0:T(8,128)(2,1)}, bf16[768,3072]{1,0:T(8,128)(2,1)}, u32[]{:S(2)}, u32[]{:S(2)}) collective-permute-start(bf16[768,3072]{1,0:T(8,128)(2,1)} %bitcast.33), channel_id=1, source_target_pairs={{0,1},{1,0},{2,3},{3,2},{4,5},{5,4},{6,7},{7,6},{8,9},{9,8},{10,11... | collective-permute-start | bytes 14155784 | tf_op jit(solution)/shard_map/ppermute | solution.py:299
  8.0 14.3 %collective-permute-start.1 = (bf16[3072,768]{1,0:T(8,128)(2,1)}, bf16[3072,768]{1,0:T(8,128)(2,1)}, u32[]{:S(2)}, u32[]{:S(2)}) collective-permute-start(bf16[3072,768]{1,0:T(8,128)(2,1)} %bitcast.36), channel_id=1, source_target_pairs={{0,1},{1,0},{2,3},{3,2},{4,5},{5,4},{6,7},{7,6},{8,9},{9,8},{10,11... | collective-permute-start | bytes 14155784 | tf_op jit(solution)/shard_map/ppermute | solution.py:300
  34.8 140.6 %all-gather.7.cloned.1.call-start = ((), (), s32[]{:S(2)}) async-start(), calls=%async_computation.5 | async-start | bytes 6684672 | tf_op jit(solution)/shard_map/all_gather | solution.py:313
  98.6 14.6 %copy-start.3 = (f32[256,1]{1,0:T(8,128)S(1)}, f32[256,1]{1,0:T(8,128)}, u32[]{:S(2)}) copy-start(f32[256,1]{1,0:T(8,128)} %get-tuple-element.16) | copy-start | bytes 3076
  112.6 100.1 %reduce-scatter.4.cloned.1.call-start = ((), (), s32[]{:S(2)}) async-start(), calls=%async_computation.6 | async-start | bytes 9732096 | tf_op jit(solution)/shard_map/reduce_scatter | solution.py:343
  196.1 19.8 %copy-start = (bf16[256,768]{1,0:T(8,128)(2,1)S(1)}, bf16[256,768]{1,0:T(8,128)(2,1)}, u32[]{:S(2)}) copy-start(bf16[256,768]{1,0:T(8,128)(2,1)} %get-tuple-element.17.g_ref) | copy-start | bytes 1179652
  196.1 19.8 %copy-start.1 = (bf16[256,768]{1,0:T(8,128)(2,1)S(1)}, bf16[256,768]{1,0:T(8,128)(2,1)}, u32[]{:S(2)}) copy-start(bf16[256,768]{1,0:T(8,128)(2,1)} %get-tuple-element.21) | copy-start | bytes 1179652
  196.1 155.7 %reduce-scatter.6.cloned.1.call-start = ((), (), s32[]{:S(2)}) async-start(), calls=%async_computation.7 | async-start | bytes 4055040 | tf_op jit(solution)/shard_map/reduce_scatter | solution.py:344
  212.7 218.9 %reduce-scatter.8.cloned.1.call-start = ((), (), s32[]{:S(2)}) async-start(), calls=%async_computation.8 | async-start | bytes 5013504 | tf_op jit(solution)/shard_map/reduce_scatter | solution.py:337
  212.7 1.8 collective-permute-start.2
  214.6 27.0 %collective-permute-start.3 = (bf16[512,768]{1,0:T(8,128)(2,1)S(1)}, bf16[512,768]{1,0:T(8,128)(2,1)S(1)}, u32[]{:S(2)}, u32[]{:S(2)}) collective-permute-start(bf16[512,768]{1,0:T(8,128)(2,1)S(1)} %pad_maximum_fusion.1), channel_id=1, source_target_pairs={{0,32},{32,64},{64,96},{96,0},{1,33},{33,65},{65,97},{97,1},{2,34}... | collective-permute-start | bytes 2359304 | tf_op jit(solution)/shard_map/ppermute | solution.py:291
  216.8 3.5 collective-permute-start.6
  217.3 29.8 %collective-permute-start.4 = (bf16[512,768]{1,0:T(8,128)(2,1)S(1)}, bf16[512,768]{1,0:T(8,128)(2,1)}, u32[]{:S(2)}, u32[]{:S(2)}) collective-permute-start(bf16[512,768]{1,0:T(8,128)(2,1)S(1)} %pad_maximum_fusion.1), channel_id=1, source_target_pairs={{0,96},{32,0},{64,32},{96,64},{1,97},{33,1},{65,33},{97,65},{2,98}... | collective-permute-start | bytes 2359304 | tf_op jit(solution)/shard_map/ppermute | solution.py:291
  218.7 56.0 %collective-permute-start.5 = (bf16[512,768]{1,0:T(8,128)(2,1)S(1)}, bf16[512,768]{1,0:T(8,128)(2,1)}, u32[]{:S(2)}, u32[]{:S(2)}) collective-permute-start(bf16[512,768]{1,0:T(8,128)(2,1)S(1)} %pad_maximum_fusion.1), channel_id=1, source_target_pairs={{0,64},{32,96},{64,0},{96,32},{1,65},{33,97},{65,1},{97,33},{2,66}... | collective-permute-start | bytes 2359304 | tf_op jit(solution)/shard_map/ppermute | solution.py:291
  220.4 72.0 %collective-permute-start.7 = (bf16[512,768]{1,0:T(8,128)(2,1)S(1)}, bf16[512,768]{1,0:T(8,128)(2,1)}, u32[]{:S(2)}, u32[]{:S(2)}) collective-permute-start(bf16[512,768]{1,0:T(8,128)(2,1)S(1)} %pad_maximum_fusion.2), channel_id=1, source_target_pairs={{0,32},{32,64},{64,96},{96,0},{1,33},{33,65},{65,97},{97,1},{2,34}... | collective-permute-start | bytes 2359304 | tf_op jit(solution)/shard_map/ppermute | solution.py:291
  220.8 75.4 %collective-permute-start.8 = (bf16[512,768]{1,0:T(8,128)(2,1)S(1)}, bf16[512,768]{1,0:T(8,128)(2,1)}, u32[]{:S(2)}, u32[]{:S(2)}) collective-permute-start(bf16[512,768]{1,0:T(8,128)(2,1)S(1)} %pad_maximum_fusion.2), channel_id=1, source_target_pairs={{0,96},{32,0},{64,32},{96,64},{1,97},{33,1},{65,33},{97,65},{2,98}... | collective-permute-start | bytes 2359304 | tf_op jit(solution)/shard_map/ppermute | solution.py:291
  241.6 71.0 %collective-permute-start.9 = (bf16[512,768]{1,0:T(8,128)(2,1)S(1)}, bf16[512,768]{1,0:T(8,128)(2,1)S(1)}, u32[]{:S(2)}, u32[]{:S(2)}) collective-permute-start(bf16[512,768]{1,0:T(8,128)(2,1)S(1)} %pad_maximum_fusion.2), channel_id=1, source_target_pairs={{0,64},{32,96},{64,0},{96,32},{1,65},{33,97},{65,1},{97,33},{2,66}... | collective-permute-start | bytes 2359304 | tf_op jit(solution)/shard_map/ppermute | solution.py:291
  276.8 36.7 %copy-start.4 = (bf16[2048,768]{1,0:T(8,128)(2,1)S(1)}, bf16[2048,768]{1,0:T(8,128)(2,1)}, u32[]{:S(2)}) copy-start(bf16[2048,768]{1,0:T(8,128)(2,1)} %constant_dynamic-update-slice_fusion) | copy-start | bytes 9437188
  313.5 5.9 %copy-start.5 = (bf16[2048,768]{1,0:T(8,128)(2,1)S(1)}, bf16[2048,768]{1,0:T(8,128)(2,1)}, u32[]{:S(2)}) copy-start(bf16[2048,768]{1,0:T(8,128)(2,1)} %constant_dynamic-update-slice_fusion) | copy-start | bytes 9437188
  351.7 86.3 %copy-start.6 = (u32[128]{0:T(128)S(1)}, u32[128]{0:T(128)}, u32[]{:S(2)}) copy-start(u32[128]{0:T(128)} %constant.91) | copy-start | bytes 1540
  351.8 86.9 %copy-start.2 = (f32[256,1]{1,0:T(8,128)S(1)}, f32[256,1]{1,0:T(8,128)}, u32[]{:S(2)}) copy-start(f32[256,1]{1,0:T(8,128)} %get-tuple-element.15) | copy-start | bytes 3076
  351.8 96.6 %all-gather.9.cloned.1.call-start = ((), (), s32[]{:S(2)}) async-start(), calls=%async_computation.9 | async-start | bytes 2433024 | tf_op jit(solution)/shard_map/all_gather | solution.py:345
  434.0 12.8 %all-to-all-start = ((f32[4,12,768]{2,1,0:T(8,128)}), f32[4,12,768]{2,1,0:T(8,128)S(1)}, u32[]{:S(2)}, u32[]{:S(2)}) async-start(f32[4,12,768]{2,1,0:T(8,128)} %reshape.126), calls=%async_computation.3 | async-start | bytes 393216 | tf_op jit(solution)/shard_map/all_to_all | solution.py:339
Sparse Core Ops, SparseCore 0:
  34.9 62.4 all-gather.4
  112.7 62.6 all-gather.6
  196.2 16.3 reduce-scatter.3
  214.9 81.3 reduce-scatter.5
  351.9 79.6 reduce-scatter.7
  433.1 15.2 all-gather.8
